TPU v7x, 32 devices: a whole 2x2x4 slice. The times are simulated.
32 devices in a mesh: groups: 2 (over x), seq: 8 (over z, y), pd: 2 (over core).
Axes of the slice: x: 2, y: 2, z: 4, core: 2. Of those that a mesh axis runs over, the one named last changes fastest.
Arguments:
- streams: bfloat16 [4096, 4, 7168], P(('groups', 'seq'), None, 'pd'), parts along dimension 0, may hold values from -6 to 6
- mix_first: bfloat16 [4, 7168, 24], P(None, 'pd'), may hold values from -0.03125 to 0.03125
- first_layer_bias: float32 [24], replicated, may hold values from -3 to 3
- pre_second: bfloat16 [4, 7168, 4], P(None, 'pd'), may hold values from -0.03125 to 0.03125
- bias_second: float32 [4], replicated, may hold values from -3 to 3
- w_latent: bfloat16 [2, 7168, 576], P(None, ('pd', 'seq')), may hold values from -0.0625 to 0.0625
- latent_gain: float32 [2, 512], replicated, may hold values from 0.5 to 1.5
- out_weight: bfloat16 [512, 7168], P(None, 'pd'), may hold values from -0.25 to 0.25
- span_slot: int32 [32], P('groups'), parts along dimension 0, may hold values from 0 to 15, each once
- block_owner: int32 [16], P('groups'), parts along dimension 0, may hold values from 0 to 7, each once
- prompt_length: int32 [2], P('groups'), parts along dimension 0, may hold values from 1024 to 2048
Outputs:
- cache: bfloat16 [2, 4096, 576], P(None, ('groups', 'seq')), parts along dimension 1
There are 2 independent parts, one for each index of `groups`. A program takes and returns all parts, laid end to end along the dimension named above; an argument that names none is the same for every part. Nothing has to cross between parts.
Inputs may be any that keep to these rules, and one draw needn't show every extreme that they name: span_slot is a permutation; slot q lies in rows q * 128 to q * 128 + 127 of streams. block_owner is a permutation.
All inputs are finite; a program needn't handle non-finite values.
Results may differ from a plain program's by a relative error of at most 0.0058.
Values may be sent and summed in bfloat16 or wider, within the bound.
A program may use at most 128 MiB of HBM per device.

v0:
```python
import jax
import jax.numpy as jnp
from jax import lax
from jax.sharding import PartitionSpec as P

LAT = 512
ROPE = 64
RESIDUAL_WAYS = 4
SINK = 20


EPSILON = 1e-06
THETA = 10000.0


def doubly_stochastic_normalize(blend_scores_raw):

    def one_sweep(turn_index, matrix):
        matrix = matrix / jnp.sum(matrix, axis=2, keepdims=True)
        return matrix / jnp.sum(matrix, axis=1, keepdims=True)

    return lax.fori_loop(0, SINK, one_sweep, jnp.exp(blend_scores_raw))


def combine(weights, stream_block):
    weighted = weights[:, 0, None] * stream_block[:, 0, :].astype(jnp.float32)
    for stream_index in range(1, RESIDUAL_WAYS):
        weighted = weighted + weights[:, stream_index, None] * stream_block[
            :, stream_index, :
        ].astype(jnp.float32)
    return weighted


def coefficients(stream_block, weights, offsets):
    flattened = stream_block.reshape(stream_block.shape[0], -1)
    partial_value = jnp.dot(
        flattened, weights.reshape(flattened.shape[1], -1), preferred_element_type=jnp.float32
    )
    elementwise_power_two = jnp.sum(jnp.square(flattened.astype(jnp.float32)), axis=1)
    projected, square_sum = lax.psum((partial_value, elementwise_power_two), "pd")
    entry_count = flattened.shape[1] * lax.axis_size("pd")
    rms_scale = jnp.sqrt(square_sum / entry_count + EPSILON)
    return projected / rms_scale[:, None] + offsets[None, :]


def cache_entry(summed, places, gain_row):
    latent = summed[:, :LAT]
    mean_square = jnp.mean(latent * latent, axis=1, keepdims=True)
    normed = latent * lax.rsqrt(mean_square + EPSILON) * gain_row[None, :]
    half_rope = ROPE // 2
    frequency = THETA ** (-jnp.arange(half_rope, dtype=jnp.float32) / half_rope)
    angles = places.astype(jnp.float32)[:, None] * frequency[None, :]
    first_half = summed[:, LAT : LAT + half_rope]
    second = summed[:, LAT + half_rope :]
    cosine_table = jnp.cos(angles)
    sine_values = jnp.sin(angles)
    rotated = jnp.concatenate(
        [
            first_half * cosine_table - second * sine_values,
            second * cosine_table + first_half * sine_values,
        ],
        axis=1,
    )
    return jnp.concatenate([normed, rotated], axis=1).astype(jnp.bfloat16)


def on_device(
    streams,
    mix_first,
    first_layer_bias,
    pre_second,
    bias_second,
    w_latent,
    latent_gain,
    out_weight,
    span_slot,
    block_owner,
    prompt_length,
):
    tokens_here = streams.shape[0]
    span_rows = tokens_here // 2
    seq_count = lax.axis_size("seq")
    my_index = lax.axis_index("seq")
    own_slots = 2 * my_index + jnp.arange(2, dtype=jnp.int32)
    span_ids = jnp.arange(2 * seq_count, dtype=jnp.int32)
    own_spans = jnp.sum(
        span_ids[None, :] * (span_slot[None, :] == own_slots[:, None]).astype(jnp.int32), axis=1
    )
    places = (
        own_spans[:, None] * span_rows + jnp.arange(span_rows, dtype=jnp.int32)[None, :]
    ).reshape(-1)
    in_prompt = places < prompt_length[0]
    my_block = jnp.sum(
        jnp.arange(seq_count, dtype=jnp.int32) * (block_owner == my_index).astype(jnp.int32)
    )
    wanted_slots = span_slot[2 * my_block + jnp.arange(2, dtype=jnp.int32)]

    def latent_of(hidden, layer_index):
        partial_value = jnp.dot(
            hidden,
            lax.all_gather(w_latent[layer_index], "seq", axis=0, tiled=True),
            preferred_element_type=jnp.float32,
        )
        summed = lax.psum(partial_value, "pd")
        return cache_entry(summed, places, latent_gain[layer_index])

    def masked(entry_rows):
        return jnp.where(in_prompt[:, None], entry_rows, jnp.zeros((), jnp.bfloat16))

    blend_weight = coefficients(streams, mix_first, first_layer_bias)
    pre_gate = jax.nn.sigmoid(blend_weight[:, :RESIDUAL_WAYS])
    post_gate = 2.0 * jax.nn.sigmoid(blend_weight[:, RESIDUAL_WAYS : 2 * RESIDUAL_WAYS])
    residual_blend_matrix = doubly_stochastic_normalize(
        blend_weight[:, 2 * RESIDUAL_WAYS :].reshape(-1, RESIDUAL_WAYS, RESIDUAL_WAYS)
    )
    hidden = combine(pre_gate, streams).astype(jnp.bfloat16)
    entry_first = latent_of(hidden, 0)
    branch = jnp.dot(entry_first[:, :LAT], out_weight, preferred_element_type=jnp.float32)
    updated = jnp.stack(
        [
            combine(residual_blend_matrix[:, stream_index, :], streams)
            + post_gate[:, stream_index, None] * branch
            for stream_index in range(RESIDUAL_WAYS)
        ],
        axis=1,
    ).astype(jnp.bfloat16)
    second_coef = coefficients(updated, pre_second, bias_second)
    hidden_second = combine(jax.nn.sigmoid(second_coef), updated).astype(jnp.bfloat16)
    entry_second = latent_of(hidden_second, 1)
    stacked = jnp.stack([masked(entry_first), masked(entry_second)])
    collected = jnp.zeros_like(stacked)
    shard_piece = lax.all_gather(stacked, "seq", axis=1, tiled=True)
    piece_rows = shard_piece.shape[1]
    span_parts = []
    for lane in range(2):
        offset = wanted_slots[lane] * span_rows
        inside = jnp.logical_and(offset >= 0, offset + span_rows <= piece_rows)
        clipped = jnp.clip(offset, 0, piece_rows - span_rows)
        sliced = lax.dynamic_slice_in_dim(shard_piece, clipped, span_rows, 1)
        span_parts.append(
            jnp.where(inside, sliced, collected[:, lane * span_rows : (lane + 1) * span_rows])
        )
    return jnp.concatenate(span_parts, axis=1)


def solution(mesh):
    placed = (
        P(("groups", "seq"), None, "pd"),
        P(None, "pd", None),
        P(),
        P(None, "pd", None),
        P(),
        P(None, ("pd", "seq"), None),
        P(),
        P(None, "pd"),
        P("groups"),
        P("groups"),
        P("groups"),
    )
    return jax.shard_map(
        on_device,
        mesh=mesh,
        in_specs=placed,
        out_specs=P(None, ("groups", "seq"), None),
        check_vma=False,
    )
```

profile of v0, /device:TPU:1, one launch (start us, length us, event | category | flops | bytes accessed | tf_op | source)
XLA Modules:
  0.0 314.8 jit_solution(10077118715863618158)
XLA Ops:
  6.5 2.4 fusion.74
  9.0 7.4 %copy.22 = bf16[256,4,3584]{2,0,1:T(8,128)(2,1)} copy(bf16[256,4,3584]{2,1,0:T(4,128)(2,1)} %param.13) | data formatting | bytes 14680064 | tf_op args[0]
  16.4 5.3 %convolution_bitcast_fusion = f32[256,24]{0,1:T(8,128)S(1)} fusion(bf16[4,3584,24]{1,2,0:T(8,128)(2,1)S(1)} %copy-done, bf16[256,4,3584]{2,1,0:T(4,128)(2,1)} %param.13), kind=kOutput, calls=%fused_computation.68 | convolution fusion | flops 176160768 | bytes 8052736 | tf_op jit(solution)/shard_map/dot_general | solution.py:36
  21.7 8.0 %multiply_reduce_fusion.1 = f32[256]{0:T(256)S(1)} fusion(bf16[256,4,3584]{2,1,0:T(4,128)(2,1)} %param.13), kind=kLoop, calls=%fused_computation.4 | loop fusion | flops 11009792 | bytes 7341056 | tf_op jit(solution)/shard_map/reduce_sum | solution.py:39
  29.7 3.4 %all-reduce.1 = (f32[256,24]{0,1:T(8,128)S(1)}, f32[256]{0:T(256)S(1)}) all-reduce(f32[256,24]{0,1:T(8,128)S(1)} %convolution_bitcast_fusion, f32[256]{0:T(256)S(1)} %multiply_reduce_fusion.1), channel_id=1, replica_groups=mesh['groups'=2,'seq'=8,'pd'=2] {'pd'}, use_global_device_ids=true, to_apply=%region_2.0 | all-reduce | flops 6400 | bytes 51200 | tf_op jit(solution)/shard_map/psum | solution.py:40
  33.2 54.7 %all-gather.8.cloned.1.call-done = bf16[1,3584,576]{2,1,0:T(8,128)(2,1)} async-done(((bf16[1,448,576]{2,1,0:T(8,128)(2,1)}), bf16[1,3584,576]{2,1,0:T(8,128)(2,1)}) %all-gather.8.cloned.1.call-update) | async-done | bytes 4128784 | tf_op jit(solution)/shard_map/all_gather | solution.py:101
  88.0 7.9 %fusion.2 = f32[256,576]{0,1:T(8,128)} fusion(bf16[1,3584,576]{2,1,0:T(8,128)(2,1)} %all-gather.8.cloned.1.call-done, f32[256]{0:T(256)S(1)} %bitcast.172, f32[256]{0:T(256)S(1)} %bitcast.171, f32[256]{0:T(256)S(1)} %bitcast.170, f32[256]{0:T(256)S(1)} %bitcast.173, bf16[256,4,3584]{2,0,1:T(8,128)(2,1)} %copy.22), kind=kOutput, calls=%fused_computation.28 | convolution fusion | flops 1067974656 | bytes 12062720 | tf_op jit(solution)/shard_map/dot_general | solution.py:99
  95.9 0.7 all-gather.10.cloned.1.call-update
  96.6 0.2 all-reduce.7.cloned.1.call-start
  96.9 1.7 while.10
  99.3 0.2 fusion.67
  99.5 15.4 %all-reduce.5.cloned.1.call-done = f32[256,576]{0,1:T(8,128)} async-done(((f32[256,576]{0,1:T(8,128)}), f32[256,576]{0,1:T(8,128)}) %all-reduce.5.cloned.1.call-update) | async-done | bytes 589840 | tf_op jit(solution)/shard_map/psum | solution.py:104
  114.9 1.1 multiply_reduce_fusion.3
  116.1 8.0 %fusion.12 = (bf16[256,3584]{1,0:T(8,128)(2,1)S(1)}, bf16[256,3584]{1,0:T(8,128)(2,1)S(1)}, f32[256,3584]{1,0:T(8,128)S(1)}) fusion(f32[256]{0:T(256)S(1)} %bitcast.160, f32[256]{0:T(256)S(1)} %bitcast.163, f32[256]{0:T(256)S(1)} %bitcast.164, f32[256]{0:T(256)S(1)} %bitcast.165, f32[256]{0:T(256)S(1)} %bitcast.162, bf16[256,4,3584]{2,0,1:T(8,128)(2,1)} %copy.22, ...), kind=kOutput, calls=%fused_computation.38 | convolution fusion | flops 961937408 | bytes 18887680 | tf_op jit(solution)/shard_map/dot_general | solution.py:118
  124.1 4.1 %fusion.17 = (bf16[256,3584]{1,0:T(8,128)(2,1)S(1)}, bf16[256,3584]{1,0:T(8,128)(2,1)S(1)}) fusion(f32[256,3584]{1,0:T(8,128)S(1)} %get-tuple-element.80, f32[256]{0:T(256)S(1)} %bitcast.151, f32[256]{0:T(256)S(1)} %bitcast.154, f32[256]{0:T(256)S(1)} %bitcast.153, f32[256]{0:T(256)S(1)} %bitcast.152, f32[256]{0:T(256)S(1)} %bitcast.155, ...), kind=kLoop, calls=%fused_computation.43 | loop fusion | flops 22020096 | bytes 14690304 | tf_op jit(solution)/shard_map/convert_element_type | solution.py:30
  128.3 2.0 fusion.38
  130.3 1.9 multiply_reduce_fusion
  132.2 2.5 all-reduce
  134.8 59.5 %all-gather.10.cloned.1.call-done = bf16[1,3584,576]{2,1,0:T(8,128)(2,1)} async-done(((bf16[1,448,576]{2,1,0:T(8,128)(2,1)}), bf16[1,3584,576]{2,1,0:T(8,128)(2,1)}) %all-gather.10.cloned.1.call-update) | async-done | bytes 4128784 | tf_op jit(solution)/shard_map/all_gather | solution.py:101
  194.3 7.4 %fusion = f32[256,576]{0,1:T(8,128)} fusion(bf16[1,3584,576]{2,1,0:T(8,128)(2,1)} %all-gather.10.cloned.1.call-done, bf16[256,3584]{1,0:T(8,128)(2,1)} %copy-done.5, bf16[256,3584]{1,0:T(8,128)(2,1)} %copy-done.2, bf16[256,3584]{1,0:T(8,128)(2,1)S(1)} %get-tuple-element.28, bf16[256,3584]{1,0:T(8,128)(2,1)} %copy-done.4, f32[256]{0:T(256)S(1)} %bitcast.175, ...), kind=kOutput, calls=%fused_computation.26 | convolution fusion | flops 1067974656 | bytes 12062720 | tf_op jit(solution)/shard_map/dot_general | solution.py:99
  201.9 0.1 fusion.72
  202.1 18.7 %all-reduce.7.cloned.1.call-done = f32[256,576]{0,1:T(8,128)} async-done(((f32[256,576]{0,1:T(8,128)}), f32[256,576]{0,1:T(8,128)}) %all-reduce.7.cloned.1.call-update) | async-done | bytes 589840 | tf_op jit(solution)/shard_map/psum | solution.py:104
  220.7 1.1 multiply_reduce_fusion.2
  221.9 1.2 fusion.39
  223.1 1.0 fusion.59
  224.2 0.9 pad_maximum_fusion.4
  225.1 0.6 fusion.68
  226.2 0.6 gather_fusion
  226.9 0.7 fusion.83
  228.8 77.0 %all-gather.6.cloned.1.call-done = bf16[2,2048,576]{1,2,0:T(8,128)(2,1)} async-done(((bf16[2,256,576]{1,2,0:T(8,128)(2,1)}), bf16[2,2048,576]{1,2,0:T(8,128)(2,1)}) %all-gather.6.cloned.1.call-update) | async-done | bytes 4718608 | tf_op jit(solution)/shard_map/all_gather | solution.py:132
  305.8 1.5 dynamic-slice_select_fusion.1
  307.4 0.9 pad_maximum_fusion.5
  (118 shorter events, 2.1 us)
Async XLA Ops:
  6.5 9.9 %copy-start = (bf16[4,3584,24]{1,2,0:T(8,128)(2,1)S(1)}, bf16[4,3584,24]{1,2,0:T(8,128)(2,1)}, u32[]{:S(2)}) copy-start(bf16[4,3584,24]{1,2,0:T(8,128)(2,1)} %param.14) | copy-start | bytes 2064388
  6.5 81.4 %all-gather.8.cloned.1.call-start = ((), (), s32[]{:S(2)}) async-start(), calls=%async_computation.3 | async-start | bytes 5160960 | tf_op jit(solution)/shard_map/all_gather | solution.py:101
  9.0 105.9 %all-reduce.5.cloned.1.call-start = ((), (), s32[]{:S(2)}) async-start(), calls=%async_computation | async-start | bytes 1179648 | tf_op jit(solution)/shard_map/psum | solution.py:104
  21.7 11.4 %copy-start.7 = (f32[24]{0:T(128)S(1)}, f32[24]{0:T(128)}, u32[]{:S(2)}) copy-start(f32[24]{0:T(128)} %param.15) | copy-start | bytes 292
  88.0 11.3 %copy-start.1 = (s32[16]{0:T(128)S(1)}, s32[16]{0:T(128)}, u32[]{:S(2)}) copy-start(s32[16]{0:T(128)} %param.21) | copy-start | bytes 196
  88.0 11.5 %copy-start.6 = (f32[2,512]{1,0:T(2,128)S(1)}, f32[2,512]{1,0:T(2,128)}, u32[]{:S(2)}) copy-start(f32[2,512]{1,0:T(2,128)} %param.19) | copy-start | bytes 12292
  95.9 98.4 %all-gather.10.cloned.1.call-start = ((), (), s32[]{:S(2)}) async-start(), calls=%async_computation.4 | async-start | bytes 5160960 | tf_op jit(solution)/shard_map/all_gather | solution.py:101
  96.6 124.1 %all-reduce.7.cloned.1.call-start = ((), (), s32[]{:S(2)}) async-start(), calls=%async_computation.1 | async-start | bytes 1179648 | tf_op jit(solution)/shard_map/psum | solution.py:104
  116.0 8.0 %slice-start = ((s8[7340032]{0:T(1024)(128)(4,1)}), s8[4194304]{0:T(1024)(128)(4,1)S(1)}, s32[]{:S(2)}) async-start(s8[7340032]{0:T(1024)(128)(4,1)} %bitcast.137), calls=%async_computation.5 | async-start | bytes 8388608
  116.0 8.0 %slice-start.1 = ((s8[7340032]{0:T(1024)(128)(4,1)}), s8[3145728]{0:T(1024)(128)(4,1)S(1)}, s32[]{:S(2)}) async-start(s8[7340032]{0:T(1024)(128)(4,1)} %bitcast.137), calls=%async_computation.6 | async-start | bytes 6291456
  124.0 6.2 %copy-start.4 = (bf16[256,3584]{1,0:T(8,128)(2,1)}, bf16[256,3584]{1,0:T(8,128)(2,1)S(1)}, u32[]{:S(2)}) copy-start(bf16[256,3584]{1,0:T(8,128)(2,1)S(1)} %get-tuple-element.26) | copy-start | bytes 5505028
  124.1 6.2 %copy-start.5 = (bf16[256,3584]{1,0:T(8,128)(2,1)}, bf16[256,3584]{1,0:T(8,128)(2,1)S(1)}, u32[]{:S(2)}) copy-start(bf16[256,3584]{1,0:T(8,128)(2,1)S(1)} %get-tuple-element.27) | copy-start | bytes 5505028
  124.1 4.2 %copy-start.9 = (bf16[4,3584,4]{1,2,0:T(4,128)(2,1)S(1)}, bf16[4,3584,4]{1,2,0:T(4,128)(2,1)}, u32[]{:S(2)}) copy-start(bf16[4,3584,4]{1,2,0:T(4,128)(2,1)} %param.16) | copy-start | bytes 344068
  128.2 2.1 copy-start.2
  130.3 4.4 %copy-start.8 = (f32[4]{0:T(128)S(1)}, f32[4]{0:T(128)}, u32[]{:S(2)}) copy-start(f32[4]{0:T(128)} %param.17) | copy-start | bytes 52
  194.3 7.7 %copy-start.3 = (f32[256,576]{0,1:T(8,128)S(1)}, f32[256,576]{0,1:T(8,128)}, u32[]{:S(2)}) copy-start(f32[256,576]{0,1:T(8,128)} %all-reduce.5.cloned.1.call-done) | copy-start | bytes 1769476
  201.7 23.4 %copy-start.10 = (s32[8]{0:T(128)S(1)}, s32[8]{0:T(128)}, u32[]{:S(2)}) copy-start(s32[8]{0:T(128)} %param.22) | copy-start | bytes 100
  201.7 104.1 %all-gather.6.cloned.1.call-start = ((), (), s32[]{:S(2)}) async-start(), calls=%async_computation.2 | async-start | bytes 5308416 | tf_op jit(solution)/shard_map/all_gather | solution.py:132
Sparse Core Ops, SparseCore 0:
  9.5 78.3 all-gather.7
  96.0 18.8 all-reduce.4
  117.1 77.1 all-gather.9
  201.8 18.8 all-reduce.6
  225.2 80.6 all-gather.5
where the time goes:
time: 317 us; the launch traced here: 315 us
  waiting for transfers between devices  226 us (71%)
  matrix products  30.6 us (10%)
  other arithmetic  24.3 us (8%)
  between operations  15.9 us (5%)
  local copies, waits for them, and re-layouts  11.2 us (4%)
  blocking collectives  5.9 us (2%)
    all_gather x2, waiting for transfers between devices, latent_of(): lax.all_gather(w_latent[layer_index], 'seq', axis=0, tiled=True)  114 us
    all_gather x1, waiting for transfers between devices, on_device(): shard_piece = lax.all_gather(stacked, 'seq', axis=1, tiled=True)  77 us
    psum x2, waiting for transfers between devices, latent_of(): summed = lax.psum(partial_value, 'pd')  34 us
    dot_general x2, matrix products, latent_of(): jnp.dot(hidden, lax.all_gather(w_latent[layer_index], 'seq', axis=0, tile...  15.3 us
    reduce_sum x2, other arithmetic, coefficients(): jnp.sum(jnp.square(flattened.astype(jnp.float32)), axis=1)  9.83 us
    dot_general x1, matrix products, on_device(): jnp.dot(entry_first[:, :LAT], out_weight, preferred_element_type=jnp.floa...  7.99 us
    unnamed x27, local copies, waits for them, and re-layouts  7.43 us
    dot_general x2, matrix products, coefficients(): jnp.dot(flattened, weights.reshape(flattened.shape[1], -1), preferred_ele...  7.32 us
  transfers between devices with their start and end apart: 5, of which 5 were waited for; matrix products, arithmetic and copies ran while one was open for 13% of the time, Pallas kernels for 0%

commit v1 on v0

v1 whole, which is shorter than its diff:
```python
import functools

import jax
import jax.numpy as jnp
from jax import lax
from jax.experimental import pallas as pl
from jax.experimental.pallas import tpu as pltpu
from jax.sharding import PartitionSpec as P

LAT = 512
ROPE = 64
RESIDUAL_WAYS = 4
SINK = 20


EPSILON = 1e-06
THETA = 10000.0


MESH = pl.DeviceIdType.MESH
LANES = 128
ROWS = 16
KV = LAT + ROPE
WIDE = LAT + LANES


def ring_position(index, count):
    return jnp.where(index % 2 == 0, index // 2, count - 1 - index // 2)


def ring_index(position, count):
    position = (position + 2 * count) % count
    return jnp.where(position < count // 2, 2 * position, 2 * (count - 1 - position) + 1)


def fused(
    count,
    streams_hbm,
    mix_hbm,
    pre_hbm,
    latent_hbm,
    out_hbm,
    table_ref,
    bias_ref,
    bias_second_ref,
    gain_ref,
    wanted_ref,
    cache_ref,
    held,
    mix,
    pre,
    weight,
    out_weight,
    branch,
    hidden,
    gate_send,
    gate_recv,
    gates,
    down_send,
    down_recv,
    entry,
    masked,
    rows_all,
    final,
    load_sems,
    ring_send,
    ring_recv,
    row_send,
    row_recv,
    pair_send,
    pair_recv,
):
    tokens = held.shape[1]
    width = held.shape[2]
    depth = latent_hbm.shape[1]
    half = tokens // 4
    me = lax.axis_index("seq")
    group = lax.axis_index("groups")
    core = lax.axis_index("pd")
    place = ring_position(me, count)
    following = ring_index(place + 1, count)
    previous = ring_index(place - 1, count)
    twin = group + 1 - 2 * (group % 2)

    to_next = {"seq": following}
    to_prev = {"seq": previous}
    to_twin = {"groups": twin}
    to_pair = {"pd": 1 - core}

    barrier = pltpu.get_barrier_semaphore()
    for target in (to_next, to_prev, to_twin, to_pair):
        pl.semaphore_signal(barrier, inc=1, device_id=target, device_id_type=MESH)
    pl.semaphore_wait(barrier, 4)

    started = []

    def send(src, dst, send_sem, recv_sem, target):
        copy = pltpu.make_async_remote_copy(
            src_ref=src,
            dst_ref=dst,
            send_sem=send_sem,
            recv_sem=recv_sem,
            device_id=target,
            device_id_type=MESH,
        )
        copy.start()
        started.append(copy)

    side = (depth // ROWS // 3) * ROWS
    middle = depth - 2 * side
    side_at = (group % 2) * (side + middle)
    other_at = (1 - group % 2) * (side + middle)

    def part(layer, owner, at, size):
        return weight.at[layer, pl.ds(pl.multiple_of(owner * depth + at, ROWS), size), :]

    def source(layer, step, owner, at, size):
        if step == 0:
            return latent_hbm.at[layer, pl.ds(pl.multiple_of(at, ROWS), size), :]
        return part(layer, owner, at, size)

    def ring_wait(layer, flow, step, dst):
        pltpu.make_async_remote_copy(
            src_ref=dst,
            dst_ref=dst,
            send_sem=ring_send.at[layer, flow, step],
            recv_sem=ring_recv.at[layer, flow, step],
            device_id=to_next,
            device_id_type=MESH,
        ).wait_recv()

    def ring_step(layer, step):
        behind = ring_index(place - step, count)
        ahead = ring_index(place + step, count)
        if step >= 1:
            ring_wait(layer, 0, step - 1, part(layer, behind, side_at, side))
        if step < count - 1:
            send(
                source(layer, step, behind, side_at, side),
                part(layer, behind, side_at, side),
                ring_send.at[layer, 0, step],
                ring_recv.at[layer, 0, step],
                to_next,
            )
        if step >= 1:
            send(
                part(layer, behind, side_at, side),
                part(layer, behind, side_at, side),
                ring_send.at[layer, 2, step - 1],
                ring_recv.at[layer, 2, step - 1],
                to_twin,
            )
            ring_wait(layer, 1, step - 1, part(layer, ahead, side, middle))
        if step < count - 1:
            send(
                source(layer, step, ahead, side, middle),
                part(layer, ahead, side, middle),
                ring_send.at[layer, 1, step],
                ring_recv.at[layer, 1, step],
                to_prev,
            )

    def twin_wait(layer):
        for step in range(count - 1):
            behind = ring_index(place - step - 1, count)
            ring_wait(layer, 2, step, part(layer, behind, other_at, side))

    progress = [0, 0]

    def advance(layer, fraction):
        goal = int(round(fraction * count))
        while progress[layer] < goal:
            ring_step(layer, progress[layer])
            progress[layer] += 1

    ring_step(0, 0)
    progress[0] = 1

    loads = []

    def load(src, dst):
        copy = pltpu.make_async_copy(src, dst, load_sems.at[len(loads)])
        copy.start()
        loads.append(copy)

    for stream in range(RESIDUAL_WAYS):
        load(streams_hbm.at[stream], held.at[stream])
    load(mix_hbm, mix)
    own_rows = pl.ds(pl.multiple_of(me * depth, ROWS), depth)
    load(latent_hbm.at[0], weight.at[0, own_rows, :])
    load(latent_hbm.at[1], weight.at[1, own_rows, :])
    load(out_hbm, out_weight)
    load(pre_hbm, pre)

    def row_block(block):
        return pl.ds(pl.multiple_of(block * ROWS, ROWS), ROWS)

    def exchange_gates(turn, projected, used):
        gate_send[turn, :, 0:used] = projected
        send(
            gate_send.at[turn],
            gate_recv.at[turn],
            pair_send.at[turn],
            pair_recv.at[turn],
            to_pair,
        )

    def gates_total(turn):
        started[-1].wait_recv()
        return (gate_send[turn] + gate_recv[turn]).T

    def scale_of(square_sum):
        return jnp.sqrt(square_sum / (2 * width * RESIDUAL_WAYS) + EPSILON)

    for copy in loads[0:RESIDUAL_WAYS]:
        copy.wait()

    def square_block(block, carry):
        rows = row_block(block)
        total = jnp.zeros((ROWS, width), jnp.float32)
        for stream in range(RESIDUAL_WAYS):
            value = held[stream, rows, :].astype(jnp.float32)
            total = total + value * value
        gate_send[0, rows, :] = jnp.broadcast_to(
            jnp.sum(total, axis=1, keepdims=True), (ROWS, LANES)
        )
        return carry

    lax.fori_loop(0, tokens // ROWS, square_block, 0)
    loads[4].wait()
    advance(0, 0.25)
    projected = jnp.dot(held[0], mix[0], preferred_element_type=jnp.float32)
    for stream in range(1, RESIDUAL_WAYS):
        projected += jnp.dot(held[stream], mix[stream], preferred_element_type=jnp.float32)
    mix_count = mix.shape[2]
    exchange_gates(0, projected, mix_count)
    turned = gates_total(0)
    advance(0, 0.5)
    coef = turned[0:mix_count] / scale_of(turned[mix_count : mix_count + 1]) + bias_ref[...]
    ways = RESIDUAL_WAYS
    gates[...] = jnp.zeros_like(gates)
    gates[0:ways, :] = jax.nn.sigmoid(coef[0:ways])
    gates[ways : 2 * ways, :] = 2.0 * jax.nn.sigmoid(coef[ways : 2 * ways])

    def sweep(turn, matrix):
        matrix = [row / jnp.sum(row, axis=0, keepdims=True) for row in matrix]
        column = matrix[0] + matrix[1] + matrix[2] + matrix[3]
        return [row / column for row in matrix]

    matrix = lax.fori_loop(
        0,
        SINK,
        sweep,
        [jnp.exp(coef[(2 + row) * ways : (3 + row) * ways]) for row in range(ways)],
    )
    for row in range(ways):
        gates[(2 + row) * ways : (3 + row) * ways, :] = matrix[row]
    gate_recv[0] = gates[...].T
    advance(0, 0.625)

    def hidden_block(turn, block, carry):
        rows = row_block(block)
        weights = gate_recv[turn, rows, :]
        total = weights[:, 0:1] * held[0, rows, :].astype(jnp.float32)
        for stream in range(1, RESIDUAL_WAYS):
            total += weights[:, stream : stream + 1] * held[stream, rows, :].astype(
                jnp.float32
            )
        hidden[rows, :] = total.astype(jnp.bfloat16)
        return carry

    lax.fori_loop(0, tokens // ROWS, functools.partial(hidden_block, 0), 0)

    def exchange_down(layer):
        twin_wait(layer)
        loads[5 + layer].wait()
        down_send[layer, :, LAT:] = jnp.zeros((tokens, LANES), jnp.float32)
        down_send[layer, :, 0:KV] = jnp.dot(
            hidden[...], weight[layer], preferred_element_type=jnp.float32
        )
        send(
            down_send.at[layer],
            down_recv.at[layer],
            pair_send.at[2 + layer],
            pair_recv.at[2 + layer],
            to_pair,
        )

    def make_entry(layer, down_copy):
        down_copy.wait_recv()
        total = down_send[layer] + down_recv[layer]
        latent = total[:, 0:LAT]
        square = jnp.mean(latent * latent, axis=1, keepdims=True)
        entry[:, 0:LAT] = (
            latent * lax.rsqrt(square + EPSILON) * gain_ref[layer : layer + 1, :]
        ).astype(jnp.bfloat16)
        key = total[:, LAT:WIDE]
        turned_key = (
            key * table_ref[0]
            + pltpu.roll(key, LANES - ROPE // 2, 1) * table_ref[1]
            + pltpu.roll(key, ROPE // 2, 1) * table_ref[2]
        )
        entry[:, LAT:KV] = turned_key[:, 0:ROPE].astype(jnp.bfloat16)
        keep = table_ref[3][:, 0:1] > 0.5
        masked[...] = jnp.where(keep, entry[...].astype(jnp.float32), 0.0).astype(jnp.bfloat16)
        for span in range(2):
            at = pl.multiple_of(span * (tokens // 2) + core * half, ROWS)
            rows_all[layer, 2 * me + span] = masked[pl.ds(at, half), :]

    def rows_of(layer, owner):
        return rows_all.at[layer, pl.ds(2 * owner, 2)]

    def row_wait(layer, flow, step, dst):
        pltpu.make_async_remote_copy(
            src_ref=dst,
            dst_ref=dst,
            send_sem=row_send.at[layer, flow, step],
            recv_sem=row_recv.at[layer, flow, step],
            device_id=to_next,
            device_id_type=MESH,
        ).wait_recv()

    def row_step(layer, step):
        for flow, sign, hops, target in (
            (0, -1, count // 2, to_next),
            (1, 1, count // 2 - 1, to_prev),
        ):
            block = rows_of(layer, ring_index(place + sign * step, count))
            if 1 <= step <= hops:
                row_wait(layer, flow, step - 1, block)
            if step < hops:
                send(
                    block,
                    block,
                    row_send.at[layer, flow, step],
                    row_recv.at[layer, flow, step],
                    target,
                )

    row_progress = [0, 0]

    def advance_rows(layer, fraction):
        goal = int(round(fraction * (count // 2 + 1)))
        while row_progress[layer] < goal:
            row_step(layer, row_progress[layer])
            row_progress[layer] += 1

    advance(0, 1.0 - 1.0 / count)
    ring_step(1, 0)
    progress[1] = 1
    advance(0, 1.0)
    exchange_down(0)
    down_copy = started[-1]
    advance(1, 0.25)
    make_entry(0, down_copy)
    advance_rows(0, 0.1)
    loads[7].wait()
    piece = width // 7
    for at in range(0, width, piece):
        branch[:, at : at + piece] = jnp.dot(
            entry[:, 0:LAT], out_weight[:, at : at + piece], preferred_element_type=jnp.float32
        )
    advance(1, 0.375)

    def update_block(block, carry):
        rows = row_block(block)
        weights = gate_recv[0, rows, :]
        squares = jnp.zeros((ROWS, 1), jnp.float32)
        step = width // 4
        for at in range(0, width, step):
            columns = slice(at, at + step)
            values = [held[j, rows, columns].astype(jnp.float32) for j in range(ways)]
            added = branch[rows, columns]
            total = jnp.zeros((ROWS, step), jnp.float32)
            for i in range(ways):
                new = weights[:, ways + i : ways + i + 1] * added
                for j in range(ways):
                    k = (2 + i) * ways + j
                    new += weights[:, k : k + 1] * values[j]
                rounded = new.astype(jnp.bfloat16)
                held[i, rows, columns] = rounded
                rounded = rounded.astype(jnp.float32)
                total += rounded * rounded
            squares += jnp.sum(total, axis=1, keepdims=True)
        gate_send[1, rows, :] = jnp.broadcast_to(squares, (ROWS, LANES))
        return carry

    lax.fori_loop(0, tokens // ROWS, update_block, 0)
    loads[8].wait()
    advance(1, 0.5)
    advance_rows(0, 0.4)
    projected = jnp.dot(held[0], pre[0], preferred_element_type=jnp.float32)
    for stream in range(1, RESIDUAL_WAYS):
        projected += jnp.dot(held[stream], pre[stream], preferred_element_type=jnp.float32)
    exchange_gates(1, projected, ways)
    turned = gates_total(1)
    advance(1, 0.625)
    coef = turned[0:ways] / scale_of(turned[ways : ways + 1]) + bias_second_ref[...]
    gates[0:ways, :] = jax.nn.sigmoid(coef)
    gate_recv[1] = gates[...].T
    advance_rows(0, 0.6)
    lax.fori_loop(0, tokens // ROWS, functools.partial(hidden_block, 1), 0)
    advance(1, 0.75)
    advance_rows(0, 0.8)
    advance(1, 0.875)
    advance_rows(0, 1.0)
    advance(1, 1.0)
    exchange_down(1)
    make_entry(1, started[-1])
    advance_rows(1, 1.0)

    for lane in range(2):
        slot = wanted_ref[lane]
        at = pl.multiple_of(lane * (tokens // 2) + core * half, ROWS)
        for layer in range(2):
            final[layer, pl.ds(at, half), :] = rows_all[layer, slot]
    lane_copies = []
    for lane in range(2):
        at = pl.multiple_of(lane * (tokens // 2) + core * half, ROWS)
        block = final.at[:, pl.ds(at, half), :]
        send(block, block, pair_send.at[4 + lane], pair_recv.at[4 + lane], to_pair)
        lane_copies.append(started[-1])
    for copy in lane_copies:
        copy.wait_recv()
    cache_ref[...] = final[...]
    for copy in started:
        copy.wait_send()


def on_device(
    streams,
    mix_first,
    first_layer_bias,
    pre_second,
    bias_second,
    w_latent,
    latent_gain,
    out_weight,
    span_slot,
    block_owner,
    prompt_length,
):
    tokens, ways, width = streams.shape
    span_rows = tokens // 2
    count = lax.axis_size("seq")
    my_index = lax.axis_index("seq")
    own_slots = 2 * my_index + jnp.arange(2, dtype=jnp.int32)
    span_ids = jnp.arange(2 * count, dtype=jnp.int32)
    own_spans = jnp.sum(
        span_ids[None, :] * (span_slot[None, :] == own_slots[:, None]).astype(jnp.int32), axis=1
    )
    places = (
        own_spans[:, None] * span_rows + jnp.arange(span_rows, dtype=jnp.int32)[None, :]
    ).reshape(-1)
    my_block = jnp.sum(
        jnp.arange(count, dtype=jnp.int32) * (block_owner == my_index).astype(jnp.int32)
    )
    wanted = jnp.sum(
        jnp.where(
            span_ids[None, :] == (2 * my_block + jnp.arange(2, dtype=jnp.int32))[:, None],
            span_slot[None, :],
            0,
        ),
        axis=1,
    )
    half_rope = ROPE // 2
    frequency = THETA ** (-jnp.arange(half_rope, dtype=jnp.float32) / half_rope)
    angles = places.astype(jnp.float32)[:, None] * frequency[None, :]
    cosine, sine = jnp.cos(angles), jnp.sin(angles)
    none = jnp.zeros_like(sine)
    keep = (places < prompt_length[0]).astype(jnp.float32)
    table = jnp.stack(
        [
            jnp.concatenate([cosine, cosine, none, none], axis=1),
            jnp.concatenate([-sine, none, none, none], axis=1),
            jnp.concatenate([none, sine, none, none], axis=1),
            jnp.broadcast_to(keep[:, None], (tokens, LANES)),
        ]
    )
    bias_rows = jnp.broadcast_to(first_layer_bias[:, None], (first_layer_bias.shape[0], tokens))
    bias_second_rows = jnp.broadcast_to(bias_second[:, None], (ways, tokens))
    any_space = pl.BlockSpec(memory_space=pl.ANY)
    vmem = pl.BlockSpec(memory_space=pltpu.VMEM)
    steps = count - 1
    return pl.pallas_call(
        functools.partial(fused, count),
        out_shape=jax.ShapeDtypeStruct((2, tokens, KV), jnp.bfloat16),
        in_specs=[any_space] * 5 + [vmem] * 4 + [pl.BlockSpec(memory_space=pltpu.SMEM)],
        out_specs=vmem,
        scratch_shapes=[
            pltpu.VMEM((ways, tokens, width), jnp.bfloat16),
            pltpu.VMEM(mix_first.shape, jnp.bfloat16),
            pltpu.VMEM(pre_second.shape, jnp.bfloat16),
            pltpu.VMEM((2, width, KV), jnp.bfloat16),
            pltpu.VMEM(out_weight.shape, jnp.bfloat16),
            pltpu.VMEM((tokens, width), jnp.float32),
            pltpu.VMEM((tokens, width), jnp.bfloat16),
            pltpu.VMEM((2, tokens, LANES), jnp.float32),
            pltpu.VMEM((2, tokens, LANES), jnp.float32),
            pltpu.VMEM((LANES, tokens), jnp.float32),
            pltpu.VMEM((2, tokens, WIDE), jnp.float32),
            pltpu.VMEM((2, tokens, WIDE), jnp.float32),
            pltpu.VMEM((tokens, KV), jnp.bfloat16),
            pltpu.VMEM((tokens, KV), jnp.bfloat16),
            pltpu.VMEM((2, 2 * count, tokens // 4, KV), jnp.bfloat16),
            pltpu.VMEM((2, tokens, KV), jnp.bfloat16),
            pltpu.SemaphoreType.DMA((9,)),
            pltpu.SemaphoreType.DMA((2, 3, steps)),
            pltpu.SemaphoreType.DMA((2, 3, steps)),
            pltpu.SemaphoreType.DMA((2, 2, count // 2)),
            pltpu.SemaphoreType.DMA((2, 2, count // 2)),
            pltpu.SemaphoreType.DMA((6,)),
            pltpu.SemaphoreType.DMA((6,)),
        ],
        compiler_params=pltpu.CompilerParams(
            collective_id=0, has_side_effects=True, vmem_limit_bytes=62 * 1024 * 1024
        ),
    )(
        jnp.transpose(streams, (1, 0, 2)),
        mix_first,
        pre_second,
        w_latent,
        out_weight,
        table,
        bias_rows,
        bias_second_rows,
        latent_gain,
        wanted,
    )


def solution(mesh):
    placed = (
        P(("groups", "seq"), None, "pd"),
        P(None, "pd", None),
        P(),
        P(None, "pd", None),
        P(),
        P(None, ("pd", "seq"), None),
        P(),
        P(None, "pd"),
        P("groups"),
        P("groups"),
        P("groups"),
    )
    return jax.shard_map(
        on_device,
        mesh=mesh,
        in_specs=placed,
        out_specs=P(None, ("groups", "seq"), None),
        check_vma=False,
    )
```

time: 317 us -> 157 us (0.50)
  waiting for transfers between devices: 226 us -> 0 us
  Pallas kernels: 0 us -> 131 us
  matrix products: 30.6 us -> 0 us
  other arithmetic: 24.3 us -> 4.47 us
  between operations: 15.9 us -> 1.44 us
  local copies, waits for them, and re-layouts: 11.2 us -> 19.5 us
  blocking collectives: 5.9 us -> 0 us
    all_gather x3 -> x0, waiting for transfers between devices: 191 us -> none  [the longest x2 114 us: latent_of(): lax.all_gather(w_latent[layer_index], 'seq', axis=0, tiled=True)]
    pallas_call x0 -> x1, Pallas kernels: none -> 131 us  [on_device(): pl.pallas_call(functools.partial(fused, count), out_shape=jax.ShapeDtypeS...]
    psum x2 -> x0, waiting for transfers between devices: 34 us -> none  [latent_of(): summed = lax.psum(partial_value, 'pd')]
    dot_general x5 -> x0, matrix products: 30.6 us -> none  [the longest x2 15.3 us: latent_of(): jnp.dot(hidden, lax.all_gather(w_latent[layer_index], 'seq', axis=0, tile...]
    reduce_sum x46 -> x2, other arithmetic: 13.7 us -> 2.8 us  [the longest x1 1.43 us: on_device(): jnp.sum(jnp.where(span_ids[None, :] == (2 * my_block + jnp.arange(2, dtyp...]
    unnamed x27 -> x5, local copies, waits for them, and re-layouts: 7.43 us -> 14.6 us
    psum x2 -> x0, blocking collectives: 5.9 us -> none  [coefficients(): lax.psum((partial_value, elementwise_power_two), 'pd')]
    convert_element_type x2, other arithmetic: 4.2 us -> 0.15 us  [the longest x1 0.07 us: on_device(): keep = (places < prompt_length[0]).astype(jnp.float32)]
  transfers between devices with their start and end apart: 5 -> 0, of which waited for: 5 -> 0; matrix products, arithmetic and copies ran while one was open for 13% -> 0% of each run, Pallas kernels for 0% -> 0%
where the time goes in v1:
time: 157 us
  Pallas kernels  131 us (83%)
  local copies, waits for them, and re-layouts  19.5 us (12%)
  other arithmetic  4.47 us (3%)
    pallas_call x1, Pallas kernels, on_device(): pl.pallas_call(functools.partial(fused, count), out_shape=jax.ShapeDtypeS...  131 us
    unnamed x5, local copies, waits for them, and re-layouts  14.6 us

profile of v1, /device:TPU:1, one launch (start us, length us, event | category | flops | bytes accessed | tf_op | source)
XLA Modules:
  0.0 156.7 jit_solution(4285826099829942912)
XLA Ops:
  0.0 0.0 copy-start
  0.7 1.4 fusion.4
  2.8 1.4 fusion.3
  4.2 0.1 fusion.2
  4.3 0.1 convert_bitcast_fusion
  4.4 0.1 pad.10.clone
  4.4 1.3 broadcast_in_dim.12.bias_second_ref
  5.8 1.3 broadcast_in_dim.11.bias_ref
  7.1 0.1 stack_broadcast_in_dim.2
  7.2 0.5 multiply_cosine_fusion
  7.7 0.1 maximum_bitcast_fusion
  7.9 0.8 pad_maximum_fusion.table_ref
  8.7 4.0 %copy.17.mix_hbm = bf16[4,3584,24]{2,1,0:T(8,128)(2,1)} copy(bf16[4,3584,24]{1,2,0:T(8,128)(2,1)} %param.12) | data formatting | bytes 1376256 | tf_op args[1]
  12.7 0.0 copy-done
  12.7 3.2 %copy.18.pre_hbm = bf16[4,3584,4]{2,1,0:T(8,128)(2,1)} copy(bf16[4,3584,4]{1,2,0:T(4,128)(2,1)S(1)} %copy-done) | data formatting | bytes 229376 | tf_op args[3]
  15.9 7.4 %copy.21 = bf16[256,4,3584]{2,0,1:T(8,128)(2,1)} copy(bf16[256,4,3584]{2,1,0:T(4,128)(2,1)} %param.11) | data formatting | bytes 14680064 | tf_op args[0]
  23.3 131.2 %shard_map.109 = bf16[2,256,576]{2,1,0:T(8,128)(2,1)} custom-call(bf16[4,256,3584]{2,1,0:T(8,128)(2,1)} %bitcast.15, bf16[4,3584,24]{2,1,0:T(8,128)(2,1)} %copy.17.mix_hbm, bf16[4,3584,4]{2,1,0:T(8,128)(2,1)} %copy.18.pre_hbm, bf16[2,448,576]{2,1,0:T(8,128)(2,1)} %latent_hbm.1, bf16[512,3584]{1,0:T(8,128)(2,1)} %out_hbm.1, ...), custom_call_target="tpu_custom_call" | custom-call | tf_op jit(solution)/shard_map/pallas_call | solution.py:485
  154.6 2.1 %copy.19 = bf16[2,256,576]{1,2,0:T(8,128)(2,1)} copy(bf16[2,256,576]{2,1,0:T(8,128)(2,1)} %shard_map.109) | data formatting | bytes 1179648 | tf_op jit(solution)/shard_map/pallas_call | solution.py:485
  (7 shorter events, 0.0 us)
Async XLA Ops:
  0.0 12.7 %copy-start = (bf16[4,3584,4]{1,2,0:T(4,128)(2,1)S(1)}, bf16[4,3584,4]{1,2,0:T(4,128)(2,1)}, u32[]{:S(2)}) copy-start(bf16[4,3584,4]{1,2,0:T(4,128)(2,1)} %param.14) | copy-start | bytes 344068

commit v2 on v1

--- a/solution.py
+++ b/solution.py
@@ -2,6 +2,7 @@
 
 import jax
 import jax.numpy as jnp
+import numpy as np
 from jax import lax
 from jax.experimental import pallas as pl
 from jax.experimental.pallas import tpu as pltpu
@@ -31,6 +32,12 @@
 def ring_index(position, count):
     position = (position + 2 * count) % count
     return jnp.where(position < count // 2, 2 * position, 2 * (count - 1 - position) + 1)
+
+
+def project(rows, columns):
+    return lax.dot_general(
+        rows, columns, (((1,), (1,)), ((), ())), preferred_element_type=jnp.float32
+    )
 
 
 def fused(
@@ -40,12 +47,18 @@
     pre_hbm,
     latent_hbm,
     out_hbm,
-    table_ref,
+    turn_ref,
+    span_ref,
     bias_ref,
     bias_second_ref,
     gain_ref,
-    wanted_ref,
+    slots_ref,
+    owners_ref,
+    length_ref,
     cache_ref,
+    table,
+    raw,
+    spread,
     held,
     mix,
     pre,
@@ -183,8 +196,10 @@
         copy.start()
         loads.append(copy)
 
-    for stream in range(RESIDUAL_WAYS):
-        load(streams_hbm.at[stream], held.at[stream])
+    quarter = tokens // RESIDUAL_WAYS
+    for piece in range(RESIDUAL_WAYS):
+        part_rows = pl.ds(piece * quarter, quarter)
+        load(streams_hbm.at[part_rows], raw.at[part_rows])
     load(mix_hbm, mix)
     own_rows = pl.ds(pl.multiple_of(me * depth, ROWS), depth)
     load(latent_hbm.at[0], weight.at[0, own_rows, :])
@@ -205,38 +220,63 @@
             to_pair,
         )
 
-    def gates_total(turn):
-        started[-1].wait_recv()
-        return (gate_send[turn] + gate_recv[turn]).T
-
-    def scale_of(square_sum):
-        return jnp.sqrt(square_sum / (2 * width * RESIDUAL_WAYS) + EPSILON)
-
-    for copy in loads[0:RESIDUAL_WAYS]:
+    def gates_total(turn, used, offsets):
+        copy = started.pop()
         copy.wait()
-
-    def square_block(block, carry):
+        total = gate_send[turn] + gate_recv[turn]
+        mean = total[:, used : used + 1] / (2 * width * RESIDUAL_WAYS)
+        scaled = total / jnp.sqrt(mean + EPSILON)
+        scaled = jnp.where(lane < used, scaled, 0.0)
+        gate_send[turn, :, :] = scaled
+        gate_send[turn, :, 0:used] = scaled[:, 0:used] + offsets
+        return gate_send[turn].T
+
+    lane = lax.broadcasted_iota(jnp.int32, (tokens, LANES), 1)
+    lane_here = lane[0 : tokens // 2]
+    row_here = lax.broadcasted_iota(jnp.int32, (tokens // 2, LANES), 0)
+    for span in range(2):
+        chosen = jnp.int32(0)
+        for candidate in range(2 * count):
+            chosen = jnp.where(slots_ref[candidate] == 2 * me + span, candidate, chosen)
+        rows = slice(span * (tokens // 2), (span + 1) * (tokens // 2))
+        base = span_ref[chosen]
+        cosine = base[0:1] * turn_ref[0] - base[1:2] * turn_ref[1]
+        sine = base[1:2] * turn_ref[0] + base[0:1] * turn_ref[1]
+        table[0, rows, :] = cosine
+        table[1, rows, :] = jnp.where(lane_here < ROPE // 2, -sine, 0.0)
+        table[2, rows, :] = jnp.where(lane_here < ROPE // 2, 0.0, sine)
+        reached = chosen * (tokens // 2) + row_here < length_ref[0]
+        table[3, rows, :] = reached.astype(jnp.float32)
+
+    def split_block(block, carry):
         rows = row_block(block)
-        total = jnp.zeros((ROWS, width), jnp.float32)
-        for stream in range(RESIDUAL_WAYS):
-            value = held[stream, rows, :].astype(jnp.float32)
-            total = total + value * value
+        total = jnp.zeros((ROWS, LANES), jnp.float32)
+        for at in range(0, width, LANES):
+            columns = slice(at, at + LANES)
+            whole = raw[rows, :, columns].astype(jnp.float32)
+            spread[at // LANES] = whole.reshape(ROWS * RESIDUAL_WAYS, LANES)
+            for stream in range(RESIDUAL_WAYS):
+                value = spread[at // LANES, pl.ds(stream, ROWS, stride=RESIDUAL_WAYS), :]
+                held[stream, rows, columns] = value.astype(jnp.bfloat16)
+                total = total + value * value
         gate_send[0, rows, :] = jnp.broadcast_to(
             jnp.sum(total, axis=1, keepdims=True), (ROWS, LANES)
         )
         return carry
 
-    lax.fori_loop(0, tokens // ROWS, square_block, 0)
+    for piece in range(RESIDUAL_WAYS):
+        loads[piece].wait()
+        blocks = quarter // ROWS
+        lax.fori_loop(piece * blocks, (piece + 1) * blocks, split_block, 0)
     loads[4].wait()
     advance(0, 0.25)
-    projected = jnp.dot(held[0], mix[0], preferred_element_type=jnp.float32)
+    projected = project(held[0], mix[0])
     for stream in range(1, RESIDUAL_WAYS):
-        projected += jnp.dot(held[stream], mix[stream], preferred_element_type=jnp.float32)
-    mix_count = mix.shape[2]
+        projected += project(held[stream], mix[stream])
+    mix_count = mix.shape[1]
     exchange_gates(0, projected, mix_count)
-    turned = gates_total(0)
+    coef = gates_total(0, mix_count, bias_ref[...])
     advance(0, 0.5)
-    coef = turned[0:mix_count] / scale_of(turned[mix_count : mix_count + 1]) + bias_ref[...]
     ways = RESIDUAL_WAYS
     gates[...] = jnp.zeros_like(gates)
     gates[0:ways, :] = jax.nn.sigmoid(coef[0:ways])
@@ -296,12 +336,12 @@
         ).astype(jnp.bfloat16)
         key = total[:, LAT:WIDE]
         turned_key = (
-            key * table_ref[0]
-            + pltpu.roll(key, LANES - ROPE // 2, 1) * table_ref[1]
-            + pltpu.roll(key, ROPE // 2, 1) * table_ref[2]
+            key * table[0]
+            + pltpu.roll(key, LANES - ROPE // 2, 1) * table[1]
+            + pltpu.roll(key, ROPE // 2, 1) * table[2]
         )
         entry[:, LAT:KV] = turned_key[:, 0:ROPE].astype(jnp.bfloat16)
-        keep = table_ref[3][:, 0:1] > 0.5
+        keep = table[3][:, 0:1] > 0.5
         masked[...] = jnp.where(keep, entry[...].astype(jnp.float32), 0.0).astype(jnp.bfloat16)
         for span in range(2):
             at = pl.multiple_of(span * (tokens // 2) + core * half, ROWS)
@@ -389,14 +429,13 @@
     loads[8].wait()
     advance(1, 0.5)
     advance_rows(0, 0.4)
-    projected = jnp.dot(held[0], pre[0], preferred_element_type=jnp.float32)
+    projected = project(held[0], pre[0])
     for stream in range(1, RESIDUAL_WAYS):
-        projected += jnp.dot(held[stream], pre[stream], preferred_element_type=jnp.float32)
+        projected += project(held[stream], pre[stream])
     exchange_gates(1, projected, ways)
-    turned = gates_total(1)
+    coef = gates_total(1, ways, bias_second_ref[...])
     advance(1, 0.625)
-    coef = turned[0:ways] / scale_of(turned[ways : ways + 1]) + bias_second_ref[...]
-    gates[0:ways, :] = jax.nn.sigmoid(coef)
+    gates[0:ways, :] = jax.nn.sigmoid(coef[0:ways])
     gate_recv[1] = gates[...].T
     advance_rows(0, 0.6)
     lax.fori_loop(0, tokens // ROWS, functools.partial(hidden_block, 1), 0)
@@ -409,8 +448,11 @@
     make_entry(1, started[-1])
     advance_rows(1, 1.0)
 
+    block_here = jnp.int32(0)
+    for block in range(count):
+        block_here = jnp.where(owners_ref[block] == me, block, block_here)
     for lane in range(2):
-        slot = wanted_ref[lane]
+        slot = slots_ref[2 * block_here + lane]
         at = pl.multiple_of(lane * (tokens // 2) + core * half, ROWS)
         for layer in range(2):
             final[layer, pl.ds(at, half), :] = rows_all[layer, slot]
@@ -443,54 +485,28 @@
     tokens, ways, width = streams.shape
     span_rows = tokens // 2
     count = lax.axis_size("seq")
-    my_index = lax.axis_index("seq")
-    own_slots = 2 * my_index + jnp.arange(2, dtype=jnp.int32)
-    span_ids = jnp.arange(2 * count, dtype=jnp.int32)
-    own_spans = jnp.sum(
-        span_ids[None, :] * (span_slot[None, :] == own_slots[:, None]).astype(jnp.int32), axis=1
-    )
-    places = (
-        own_spans[:, None] * span_rows + jnp.arange(span_rows, dtype=jnp.int32)[None, :]
-    ).reshape(-1)
-    my_block = jnp.sum(
-        jnp.arange(count, dtype=jnp.int32) * (block_owner == my_index).astype(jnp.int32)
-    )
-    wanted = jnp.sum(
-        jnp.where(
-            span_ids[None, :] == (2 * my_block + jnp.arange(2, dtype=jnp.int32))[:, None],
-            span_slot[None, :],
-            0,
-        ),
-        axis=1,
-    )
-    half_rope = ROPE // 2
-    frequency = THETA ** (-jnp.arange(half_rope, dtype=jnp.float32) / half_rope)
-    angles = places.astype(jnp.float32)[:, None] * frequency[None, :]
-    cosine, sine = jnp.cos(angles), jnp.sin(angles)
-    none = jnp.zeros_like(sine)
-    keep = (places < prompt_length[0]).astype(jnp.float32)
-    table = jnp.stack(
-        [
-            jnp.concatenate([cosine, cosine, none, none], axis=1),
-            jnp.concatenate([-sine, none, none, none], axis=1),
-            jnp.concatenate([none, sine, none, none], axis=1),
-            jnp.broadcast_to(keep[:, None], (tokens, LANES)),
-        ]
-    )
-    bias_rows = jnp.broadcast_to(first_layer_bias[:, None], (first_layer_bias.shape[0], tokens))
-    bias_second_rows = jnp.broadcast_to(bias_second[:, None], (ways, tokens))
+    frequency = THETA ** (-(np.arange(LANES) % (ROPE // 2)) / (ROPE // 2))
+    used = np.arange(LANES) < ROPE
+    row_angles = np.arange(span_rows)[:, None] * frequency
+    span_angles = np.arange(2 * count)[:, None] * span_rows * frequency
+    turns = np.stack([np.cos(row_angles) * used, np.sin(row_angles) * used])
+    span_turns = np.stack([np.cos(span_angles), np.sin(span_angles)], axis=1)
     any_space = pl.BlockSpec(memory_space=pl.ANY)
     vmem = pl.BlockSpec(memory_space=pltpu.VMEM)
+    smem = pl.BlockSpec(memory_space=pltpu.SMEM)
     steps = count - 1
     return pl.pallas_call(
         functools.partial(fused, count),
         out_shape=jax.ShapeDtypeStruct((2, tokens, KV), jnp.bfloat16),
-        in_specs=[any_space] * 5 + [vmem] * 4 + [pl.BlockSpec(memory_space=pltpu.SMEM)],
+        in_specs=[any_space] * 5 + [vmem] * 5 + [smem] * 3,
         out_specs=vmem,
         scratch_shapes=[
+            pltpu.VMEM((4, tokens, LANES), jnp.float32),
+            pltpu.VMEM((tokens, ways, width), jnp.bfloat16),
+            pltpu.VMEM((width // LANES, ROWS * ways, LANES), jnp.float32),
             pltpu.VMEM((ways, tokens, width), jnp.bfloat16),
-            pltpu.VMEM(mix_first.shape, jnp.bfloat16),
-            pltpu.VMEM(pre_second.shape, jnp.bfloat16),
+            pltpu.VMEM((ways, mix_first.shape[2], width), jnp.bfloat16),
+            pltpu.VMEM((ways, pre_second.shape[2], width), jnp.bfloat16),
             pltpu.VMEM((2, width, KV), jnp.bfloat16),
             pltpu.VMEM(out_weight.shape, jnp.bfloat16),
             pltpu.VMEM((tokens, width), jnp.float32),
@@ -516,16 +532,19 @@
             collective_id=0, has_side_effects=True, vmem_limit_bytes=62 * 1024 * 1024
         ),
     )(
-        jnp.transpose(streams, (1, 0, 2)),
-        mix_first,
-        pre_second,
+        streams,
+        jnp.swapaxes(mix_first, 1, 2),
+        jnp.swapaxes(pre_second, 1, 2),
         w_latent,
         out_weight,
-        table,
-        bias_rows,
-        bias_second_rows,
+        turns.astype(np.float32),
+        span_turns.astype(np.float32),
+        first_layer_bias[None, :],
+        bias_second[None, :],
         latent_gain,
-        wanted,
+        span_slot,
+        block_owner,
+        prompt_length,
     )
 
 

time: 157 us -> 137 us (0.87)
  local copies, waits for them, and re-layouts: 19.5 us -> 2.14 us
  other arithmetic: 4.47 us -> 0 us
  Pallas kernels: 131 us -> 134 us
    unnamed x5 -> x0, local copies, waits for them, and re-layouts: 14.6 us -> none
    reduce_sum x2 -> x0, other arithmetic: 2.8 us -> none  [the longest x1 1.43 us: on_device(): jnp.sum(jnp.where(span_ids[None, :] == (2 * my_block + jnp.arange(2, dtyp...]
    pallas_call x1, Pallas kernels: 131 us -> 134 us  [on_device(): pl.pallas_call(functools.partial(fused, count), out_shape=jax.ShapeDtypeS...]
    broadcast_in_dim x3 -> x0, local copies, waits for them, and re-layouts: 2.64 us -> none  [the longest x1 1.32 us: on_device(): jnp.broadcast_to(first_layer_bias[:, None], (first_layer_bias.shape[0], t...]
where the time goes in v2:
time: 137 us
  Pallas kernels  134 us (98%)
  local copies, waits for them, and re-layouts  2.14 us (2%)
    pallas_call x1, Pallas kernels, on_device(): pl.pallas_call(functools.partial(fused, count), out_shape=jax.ShapeDtypeS...  134 us

profile of v2, /device:TPU:1, one launch (start us, length us, event | category | flops | bytes accessed | tf_op | source)
XLA Modules:
  0.0 136.8 jit_solution(5273704231599599292)
XLA Ops:
  0.7 134.0 %shard_map.127 = bf16[2,256,576]{2,1,0:T(8,128)(2,1)} custom-call(bf16[256,4,3584]{2,1,0:T(4,128)(2,1)} %streams_hbm.1, bf16[4,24,3584]{2,1,0:T(8,128)(2,1)} %bitcast.4, bf16[4,4,3584]{2,1,0:T(4,128)(2,1)} %bitcast.5, bf16[2,448,576]{2,1,0:T(8,128)(2,1)} %latent_hbm.1, bf16[512,3584]{1,0:T(8,128)(2,1)} %out_hbm.1, f32[2,128,128]{2,1,0:T(8,128)} %constant.4.clone.turn_ref, ...), custom_call_target="tpu_custom_call" | custom-call | tf_op jit(solution)/shard_map/pallas_call | solution.py:498
  134.7 2.1 %copy.14 = bf16[2,256,576]{1,2,0:T(8,128)(2,1)} copy(bf16[2,256,576]{2,1,0:T(8,128)(2,1)} %shard_map.127) | data formatting | bytes 1179648 | tf_op jit(solution)/shard_map/pallas_call | solution.py:498
